TPU v7x, 512 devices: a whole 4x8x8 slice. The times are simulated.
512 devices in a mesh: cols: 64 (over z, x, y_hi), rows: 8 (over y_lo, core).
Axes of the slice: x: 4, y: 8 (y_hi: 2, y_lo: 4; y = y_hi * 4 + y_lo), z: 8, core: 2. Of those that a mesh axis runs over, the one named last changes fastest.
Arguments:
- vectors: float32 [8192, 16384], P('rows', 'cols'), may hold values from -6 to 6
- reflectors: float32 [15, 1024, 512], P(None, None, 'cols'), may hold values from -40 to 40, as said below
- factors: float32 [15, 512, 512], P(None, None, 'cols'), may hold values from -1 to 1
Outputs:
- result: float32 [8192, 16384], P('rows', 'cols')
Inputs may be any that keep to these rules, and one draw needn't show every extreme that they name: `reflectors`: column j of each block is zero outside its rows j to j + 511, and its entry in row j is 1.
All inputs are finite; a program needn't handle non-finite values.
Results may differ from a plain program's by a relative error of at most 0.00028.
Values sent between devices are 32-bit elements; how exact they have to be, the bound alone decides.
A program may use at most 64 MiB of HBM per device.

v0:
```python
import jax
import jax.numpy as jnp
from jax import lax
from jax.sharding import PartitionSpec as P


def rows_first(arrays, axis, dims):
    turned = [jnp.moveaxis(a, dim, 0) for a, dim in zip(arrays, dims)]
    both = jnp.concatenate([t.reshape(len(t), -1) for t in turned], axis=1)
    filled, at, outs = (lax.all_gather(both, axis, axis=0, tiled=True), 0, [])
    for t, dim in zip(turned, dims):
        slab = filled[:, at : at + t[0].size].reshape(-1, *t.shape[1:])
        outs.append(jnp.moveaxis(slab, 0, dim))
        at += t[0].size
    return tuple(outs)


def shifted(value, axis, by):
    length = lax.axis_size(axis)
    pairs = [(i, i + by) for i in range(length) if 0 <= i + by < length]
    return lax.ppermute(value, axis, pairs)


def reflect(window, basis_cols, factor):
    highest = lax.Precision.HIGHEST
    weights = lax.dot_general(
        basis_cols,
        window,
        (((0,), (0,)), ((), ())),
        precision=highest,
        preferred_element_type=jnp.float32,
    )
    coeffs = jnp.dot(factor, weights, precision=highest, preferred_element_type=jnp.float32)
    return window - jnp.dot(
        basis_cols, coeffs, precision=highest, preferred_element_type=jnp.float32
    )


def body(vectors, reflectors, factors):
    row_count = lax.axis_size("rows")
    row_index = lax.axis_index("rows")
    rows_dev, cols_dev = vectors.shape
    half_rows = rows_dev // 2
    first_index = jnp.maximum(2 * row_index - 1, 0)
    own_index = 2 * row_index
    upper_basis = lax.dynamic_index_in_dim(reflectors, first_index, 0, keepdims=False)
    upper_factor = lax.dynamic_index_in_dim(factors, first_index, 0, keepdims=False)
    own_basis = lax.dynamic_index_in_dim(reflectors, own_index, 0, keepdims=False)
    own_factor = lax.dynamic_index_in_dim(factors, own_index, 0, keepdims=False)
    pair_basis = jnp.stack([upper_basis, own_basis])
    pair_factor = jnp.stack([upper_factor, own_factor])
    full_basis, full_factor = rows_first((pair_basis, pair_factor), "cols", (2, 2))
    upper_basis, own_basis = (full_basis[0], full_basis[1])
    upper_factor, own_factor = (full_factor[0], full_factor[1])
    stripe_count = 2
    stripe_cols = cols_dev // stripe_count
    has_upper = row_index > 0
    has_lower = row_index < row_count - 1

    def process(state_now, incoming, stripe_index):
        matrix, outgoing, returning = state_now
        start = stripe_index * stripe_cols
        stripe = lax.dynamic_slice_in_dim(matrix, start, stripe_cols, 1)
        window = reflect(
            jnp.concatenate([incoming, stripe[:half_rows]], 0), upper_basis, upper_factor
        )
        upper_rows = jnp.where(has_upper, window[half_rows:], stripe[:half_rows])
        stripe = reflect(
            jnp.concatenate([upper_rows, stripe[half_rows:]], 0), own_basis, own_factor
        )
        matrix = lax.dynamic_update_slice_in_dim(matrix, stripe, start, 1)
        return (matrix, stripe[half_rows:], window[:half_rows])

    def advance(turn_index, state_now):
        matrix, outgoing, returning = state_now
        incoming = shifted(outgoing, "rows", 1)
        arrived = shifted(returning, "rows", -1)
        late_stripe = turn_index - row_index - 2
        landing = (late_stripe >= 0) & (late_stripe < stripe_count) & has_lower
        late_start = jnp.clip(late_stripe, 0, stripe_count - 1) * stripe_cols
        current = lax.dynamic_slice(matrix, (half_rows, late_start), (half_rows, stripe_cols))
        matrix = lax.dynamic_update_slice(
            matrix, jnp.where(landing, arrived, current), (half_rows, late_start)
        )
        stripe_index = turn_index - row_index
        is_active = (stripe_index >= 0) & (stripe_index < stripe_count)
        safe_index = jnp.clip(stripe_index, 0, stripe_count - 1)

        def busy(state_in):
            return process(state_in, incoming, safe_index)

        def resting(state_in):
            return state_in

        return lax.cond(is_active, busy, resting, (matrix, outgoing, returning))

    blank = jnp.zeros((half_rows, stripe_cols), jnp.float32)
    matrix, outgoing, returning = lax.fori_loop(
        0, row_count + stripe_count, advance, (vectors, blank, blank)
    )
    return matrix


def solution(mesh):
    placed = (P("rows", "cols"), P(None, None, "cols"), P(None, None, "cols"))
    return jax.shard_map(
        body, mesh=mesh, in_specs=placed, out_specs=P("rows", "cols"), check_vma=False
    )
```

profile of v0, /device:TPU:27, one launch (start us, length us, event | category | flops | bytes accessed | tf_op | source)
XLA Modules:
  0.0 437.3 jit_solution(806147630762032506)
XLA Ops:
  8.8 2.6 copy.8
  11.3 166.1 %all-gather.2.cloned.1.call-done = f32[512,3072]{1,0:T(8,128)} async-done(((f32[8,3072]{1,0:T(8,128)}), f32[512,3072]{1,0:T(8,128)}) %all-gather.2.cloned.1.call-update) | async-done | bytes 6291472 | tf_op jit(solution)/shard_map/all_gather | solution.py:10
  177.5 4.8 %slice.43 = f32[512,2048]{1,0:T(8,128)} slice(f32[512,3072]{1,0:T(8,128)} %all-gather.2.cloned.1.call-done), slice={[0:512], [0:2048]} | slice | bytes 8388608 | tf_op jit(solution)/shard_map/slice | solution.py:12
  182.2 5.4 %copy.10 = f32[512,2048]{0,1:T(8,128)} copy(f32[512,2048]{1,0:T(8,128)} %slice.43) | data formatting | bytes 8388608 | tf_op jit(solution)/shard_map/reshape | solution.py:12
  187.6 3.2 slice.45
  190.8 1.9 copy.11
  195.3 1.8 slice_bitcast_fusion
  198.5 229.4 %while.19 = (s32[]{:T(128)}, f32[1024,256]{0,1:T(8,128)}, f32[512,128]{0,1:T(8,128)}, f32[512,128]{0,1:T(8,128)}, s32[]{:T(128)}, /*index=5*/pred[]{:T(512)}, pr...) while((s32[]{:T(128)}, f32[1024,256]{0,1:T(8,128)}, ...), condition=%wide.region_3.4_spmd, body=%wide.region_0.3_spmd.sunk | while | flops 4027449344 | bytes 42992328 | solution.py:98
  198.5 6.7 %collective-permute-start = (f32[512,128]{0,1:T(8,128)}, f32[512,128]{0,1:T(8,128)}, u32[]{:S(2)}, u32[]{:S(2)}) collective-permute-start(f32[512,128]{0,1:T(8,128)} %get-tuple-element.479), channel_id=1, source_target_pairs={{1,0},{2,1},{3,2},{4,3},{5,4},{6,5},{7,6},{9,8},{10,9},{11,10},{12... | collective-permute-start | bytes 786440 | tf_op jit(solution)/shard_map/while/body/eval_jaxpr/ppermute | solution.py:21
  206.6 1.7 select_dynamic-update-slice_fusion.2
  208.3 2.2 collective-permute-done.1
  210.5 9.6 %collective-permute-start = (f32[512,128]{0,1:T(8,128)}, f32[512,128]{0,1:T(8,128)}, u32[]{:S(2)}, u32[]{:S(2)}) collective-permute-start(f32[512,128]{0,1:T(8,128)} %get-tuple-element.479), channel_id=1, source_target_pairs={{1,0},{2,1},{3,2},{4,3},{5,4},{6,5},{7,6},{9,8},{10,9},{11,10},{12... | collective-permute-start | bytes 786440 | tf_op jit(solution)/shard_map/while/body/eval_jaxpr/ppermute | solution.py:21
  223.8 6.2 %collective-permute-start = (f32[512,128]{0,1:T(8,128)}, f32[512,128]{0,1:T(8,128)}, u32[]{:S(2)}, u32[]{:S(2)}) collective-permute-start(f32[512,128]{0,1:T(8,128)} %get-tuple-element.479), channel_id=1, source_target_pairs={{1,0},{2,1},{3,2},{4,3},{5,4},{6,5},{7,6},{9,8},{10,9},{11,10},{12... | collective-permute-start | bytes 786440 | tf_op jit(solution)/shard_map/while/body/eval_jaxpr/ppermute | solution.py:21
  233.6 6.2 %collective-permute-start = (f32[512,128]{0,1:T(8,128)}, f32[512,128]{0,1:T(8,128)}, u32[]{:S(2)}, u32[]{:S(2)}) collective-permute-start(f32[512,128]{0,1:T(8,128)} %get-tuple-element.479), channel_id=1, source_target_pairs={{1,0},{2,1},{3,2},{4,3},{5,4},{6,5},{7,6},{9,8},{10,9},{11,10},{12... | collective-permute-start | bytes 786440 | tf_op jit(solution)/shard_map/while/body/eval_jaxpr/ppermute | solution.py:21
  243.4 16.7 %collective-permute-start = (f32[512,128]{0,1:T(8,128)}, f32[512,128]{0,1:T(8,128)}, u32[]{:S(2)}, u32[]{:S(2)}) collective-permute-start(f32[512,128]{0,1:T(8,128)} %get-tuple-element.479), channel_id=1, source_target_pairs={{1,0},{2,1},{3,2},{4,3},{5,4},{6,5},{7,6},{9,8},{10,9},{11,10},{12... | collective-permute-start | bytes 786440 | tf_op jit(solution)/shard_map/while/body/eval_jaxpr/ppermute | solution.py:21
  263.2 7.7 %collective-permute-done.1 = f32[512,128]{0,1:T(8,128)S(1)} collective-permute-done((f32[512,128]{0,1:T(8,128)}, f32[512,128]{0,1:T(8,128)S(1)}, u32[]{:S(2)}, u32[]{:S(2)}) %collective-permute-start.1) | collective-permute-done | bytes 262176 | tf_op jit(solution)/shard_map/while/body/eval_jaxpr/ppermute | solution.py:21
  270.9 28.4 %collective-permute-start = (f32[512,128]{0,1:T(8,128)}, f32[512,128]{0,1:T(8,128)}, u32[]{:S(2)}, u32[]{:S(2)}) collective-permute-start(f32[512,128]{0,1:T(8,128)} %get-tuple-element.479), channel_id=1, source_target_pairs={{1,0},{2,1},{3,2},{4,3},{5,4},{6,5},{7,6},{9,8},{10,9},{11,10},{12... | collective-permute-start | bytes 786440 | tf_op jit(solution)/shard_map/while/body/eval_jaxpr/ppermute | solution.py:21
  302.3 10.7 %collective-permute-done.1 = f32[512,128]{0,1:T(8,128)S(1)} collective-permute-done((f32[512,128]{0,1:T(8,128)}, f32[512,128]{0,1:T(8,128)S(1)}, u32[]{:S(2)}, u32[]{:S(2)}) %collective-permute-start.1) | collective-permute-done | bytes 262176 | tf_op jit(solution)/shard_map/while/body/eval_jaxpr/ppermute | solution.py:21
  313.0 26.0 %collective-permute-start = (f32[512,128]{0,1:T(8,128)}, f32[512,128]{0,1:T(8,128)}, u32[]{:S(2)}, u32[]{:S(2)}) collective-permute-start(f32[512,128]{0,1:T(8,128)} %get-tuple-element.479), channel_id=1, source_target_pairs={{1,0},{2,1},{3,2},{4,3},{5,4},{6,5},{7,6},{9,8},{10,9},{11,10},{12... | collective-permute-start | bytes 786440 | tf_op jit(solution)/shard_map/while/body/eval_jaxpr/ppermute | solution.py:21
  342.1 13.7 %collective-permute-done.1 = f32[512,128]{0,1:T(8,128)S(1)} collective-permute-done((f32[512,128]{0,1:T(8,128)}, f32[512,128]{0,1:T(8,128)S(1)}, u32[]{:S(2)}, u32[]{:S(2)}) %collective-permute-start.1) | collective-permute-done | bytes 262176 | tf_op jit(solution)/shard_map/while/body/eval_jaxpr/ppermute | solution.py:21
  355.8 23.0 %collective-permute-start = (f32[512,128]{0,1:T(8,128)}, f32[512,128]{0,1:T(8,128)}, u32[]{:S(2)}, u32[]{:S(2)}) collective-permute-start(f32[512,128]{0,1:T(8,128)} %get-tuple-element.479), channel_id=1, source_target_pairs={{1,0},{2,1},{3,2},{4,3},{5,4},{6,5},{7,6},{9,8},{10,9},{11,10},{12... | collective-permute-start | bytes 786440 | tf_op jit(solution)/shard_map/while/body/eval_jaxpr/ppermute | solution.py:21
  382.5 15.0 %conditional.2 = ((f32[1024,256]{0,1:T(8,128)}, f32[512,128]{0,1:T(8,128)}, f32[512,128]{0,1:T(8,128)})) conditional(s32[]{:T(128)} %convert_element_type.11, (f32[1024,256]{0,1:T(8,128)}, f32[512,128]{0,1:T(8,128)}, f32[512,128]{0,1:T(8,128)}) %tuple.54, (pred[]{:T(512)}, s32[]{:T(128)}, f32[1024,256]{0,1:T(8,128)}, f32[512,128]{0,1:T(8,128)S(1)}, ...), branch_computations={%region_1.1_spmd, %region_2.2_spmd} | conditional | flops 4027383808 | bytes 40108272 | solution.py:95
  383.7 3.0 fusion.3
  387.9 2.3 fusion
  393.4 2.3 constant_dynamic-update-slice_fusion
  397.5 6.2 %collective-permute-start = (f32[512,128]{0,1:T(8,128)}, f32[512,128]{0,1:T(8,128)}, u32[]{:S(2)}, u32[]{:S(2)}) collective-permute-start(f32[512,128]{0,1:T(8,128)} %get-tuple-element.479), channel_id=1, source_target_pairs={{1,0},{2,1},{3,2},{4,3},{5,4},{6,5},{7,6},{9,8},{10,9},{11,10},{12... | collective-permute-start | bytes 786440 | tf_op jit(solution)/shard_map/while/body/eval_jaxpr/ppermute | solution.py:21
  407.3 15.0 %conditional.2 = ((f32[1024,256]{0,1:T(8,128)}, f32[512,128]{0,1:T(8,128)}, f32[512,128]{0,1:T(8,128)})) conditional(s32[]{:T(128)} %convert_element_type.11, (f32[1024,256]{0,1:T(8,128)}, f32[512,128]{0,1:T(8,128)}, f32[512,128]{0,1:T(8,128)}) %tuple.54, (pred[]{:T(512)}, s32[]{:T(128)}, f32[1024,256]{0,1:T(8,128)}, f32[512,128]{0,1:T(8,128)S(1)}, ...), branch_computations={%region_1.1_spmd, %region_2.2_spmd} | conditional | flops 4027383808 | bytes 40108272 | solution.py:95
  408.5 3.0 fusion.3
  412.7 2.3 fusion
  418.2 2.3 constant_dynamic-update-slice_fusion
  422.3 2.0 collective-permute-start
  427.9 2.5 copy.9
  (83 shorter events, 52.5 us)
Async XLA Ops:
  6.5 170.9 %all-gather.2.cloned.1.call-start = ((), (), s32[]{:S(2)}) async-start(), calls=%async_computation | async-start | bytes 6389760 | tf_op jit(solution)/shard_map/all_gather | solution.py:10
  192.7 2.6 copy-start.4
  198.5 8.1 %collective-permute-start = (f32[512,128]{0,1:T(8,128)}, f32[512,128]{0,1:T(8,128)}, u32[]{:S(2)}, u32[]{:S(2)}) collective-permute-start(f32[512,128]{0,1:T(8,128)} %get-tuple-element.479), channel_id=1, source_target_pairs={{1,0},{2,1},{3,2},{4,3},{5,4},{6,5},{7,6},{9,8},{10,9},{11,10},{12... | collective-permute-start | bytes 786440 | tf_op jit(solution)/shard_map/while/body/eval_jaxpr/ppermute | solution.py:21
  205.2 5.3 %collective-permute-start.1 = (f32[512,128]{0,1:T(8,128)}, f32[512,128]{0,1:T(8,128)S(1)}, u32[]{:S(2)}, u32[]{:S(2)}) collective-permute-start(f32[512,128]{0,1:T(8,128)} %get-tuple-element.478), channel_id=1, source_target_pairs={{0,1},{1,2},{2,3},{3,4},{4,5},{5,6},{6,7},{8,9},{9,10},{10,11},{11... | collective-permute-start | bytes 786440 | tf_op jit(solution)/shard_map/while/body/eval_jaxpr/ppermute | solution.py:21
  210.5 10.9 %collective-permute-start = (f32[512,128]{0,1:T(8,128)}, f32[512,128]{0,1:T(8,128)}, u32[]{:S(2)}, u32[]{:S(2)}) collective-permute-start(f32[512,128]{0,1:T(8,128)} %get-tuple-element.479), channel_id=1, source_target_pairs={{1,0},{2,1},{3,2},{4,3},{5,4},{6,5},{7,6},{9,8},{10,9},{11,10},{12... | collective-permute-start | bytes 786440 | tf_op jit(solution)/shard_map/while/body/eval_jaxpr/ppermute | solution.py:21
  220.2 3.6 collective-permute-start.1
  223.8 7.5 %collective-permute-start = (f32[512,128]{0,1:T(8,128)}, f32[512,128]{0,1:T(8,128)}, u32[]{:S(2)}, u32[]{:S(2)}) collective-permute-start(f32[512,128]{0,1:T(8,128)} %get-tuple-element.479), channel_id=1, source_target_pairs={{1,0},{2,1},{3,2},{4,3},{5,4},{6,5},{7,6},{9,8},{10,9},{11,10},{12... | collective-permute-start | bytes 786440 | tf_op jit(solution)/shard_map/while/body/eval_jaxpr/ppermute | solution.py:21
  230.0 3.6 collective-permute-start.1
  233.6 7.5 %collective-permute-start = (f32[512,128]{0,1:T(8,128)}, f32[512,128]{0,1:T(8,128)}, u32[]{:S(2)}, u32[]{:S(2)}) collective-permute-start(f32[512,128]{0,1:T(8,128)} %get-tuple-element.479), channel_id=1, source_target_pairs={{1,0},{2,1},{3,2},{4,3},{5,4},{6,5},{7,6},{9,8},{10,9},{11,10},{12... | collective-permute-start | bytes 786440 | tf_op jit(solution)/shard_map/while/body/eval_jaxpr/ppermute | solution.py:21
  239.8 3.6 collective-permute-start.1
  243.4 18.0 %collective-permute-start = (f32[512,128]{0,1:T(8,128)}, f32[512,128]{0,1:T(8,128)}, u32[]{:S(2)}, u32[]{:S(2)}) collective-permute-start(f32[512,128]{0,1:T(8,128)} %get-tuple-element.479), channel_id=1, source_target_pairs={{1,0},{2,1},{3,2},{4,3},{5,4},{6,5},{7,6},{9,8},{10,9},{11,10},{12... | collective-permute-start | bytes 786440 | tf_op jit(solution)/shard_map/while/body/eval_jaxpr/ppermute | solution.py:21
  260.1 10.7 %collective-permute-start.1 = (f32[512,128]{0,1:T(8,128)}, f32[512,128]{0,1:T(8,128)S(1)}, u32[]{:S(2)}, u32[]{:S(2)}) collective-permute-start(f32[512,128]{0,1:T(8,128)} %get-tuple-element.478), channel_id=1, source_target_pairs={{0,1},{1,2},{2,3},{3,4},{4,5},{5,6},{6,7},{8,9},{9,10},{10,11},{11... | collective-permute-start | bytes 786440 | tf_op jit(solution)/shard_map/while/body/eval_jaxpr/ppermute | solution.py:21
  270.9 29.7 %collective-permute-start = (f32[512,128]{0,1:T(8,128)}, f32[512,128]{0,1:T(8,128)}, u32[]{:S(2)}, u32[]{:S(2)}) collective-permute-start(f32[512,128]{0,1:T(8,128)} %get-tuple-element.479), channel_id=1, source_target_pairs={{1,0},{2,1},{3,2},{4,3},{5,4},{6,5},{7,6},{9,8},{10,9},{11,10},{12... | collective-permute-start | bytes 786440 | tf_op jit(solution)/shard_map/while/body/eval_jaxpr/ppermute | solution.py:21
  299.3 13.8 %collective-permute-start.1 = (f32[512,128]{0,1:T(8,128)}, f32[512,128]{0,1:T(8,128)S(1)}, u32[]{:S(2)}, u32[]{:S(2)}) collective-permute-start(f32[512,128]{0,1:T(8,128)} %get-tuple-element.478), channel_id=1, source_target_pairs={{0,1},{1,2},{2,3},{3,4},{4,5},{5,6},{6,7},{8,9},{9,10},{10,11},{11... | collective-permute-start | bytes 786440 | tf_op jit(solution)/shard_map/while/body/eval_jaxpr/ppermute | solution.py:21
  313.0 27.4 %collective-permute-start = (f32[512,128]{0,1:T(8,128)}, f32[512,128]{0,1:T(8,128)}, u32[]{:S(2)}, u32[]{:S(2)}) collective-permute-start(f32[512,128]{0,1:T(8,128)} %get-tuple-element.479), channel_id=1, source_target_pairs={{1,0},{2,1},{3,2},{4,3},{5,4},{6,5},{7,6},{9,8},{10,9},{11,10},{12... | collective-permute-start | bytes 786440 | tf_op jit(solution)/shard_map/while/body/eval_jaxpr/ppermute | solution.py:21
  339.1 16.8 %collective-permute-start.1 = (f32[512,128]{0,1:T(8,128)}, f32[512,128]{0,1:T(8,128)S(1)}, u32[]{:S(2)}, u32[]{:S(2)}) collective-permute-start(f32[512,128]{0,1:T(8,128)} %get-tuple-element.478), channel_id=1, source_target_pairs={{0,1},{1,2},{2,3},{3,4},{4,5},{5,6},{6,7},{8,9},{9,10},{10,11},{11... | collective-permute-start | bytes 786440 | tf_op jit(solution)/shard_map/while/body/eval_jaxpr/ppermute | solution.py:21
  355.8 24.3 %collective-permute-start = (f32[512,128]{0,1:T(8,128)}, f32[512,128]{0,1:T(8,128)}, u32[]{:S(2)}, u32[]{:S(2)}) collective-permute-start(f32[512,128]{0,1:T(8,128)} %get-tuple-element.479), channel_id=1, source_target_pairs={{1,0},{2,1},{3,2},{4,3},{5,4},{6,5},{7,6},{9,8},{10,9},{11,10},{12... | collective-permute-start | bytes 786440 | tf_op jit(solution)/shard_map/while/body/eval_jaxpr/ppermute | solution.py:21
  378.9 3.6 collective-permute-start.1
  382.5 4.2 copy-start.1
  383.6 4.2 copy-start
  390.9 2.5 copy-start.2
  395.8 1.0 copy-start.3
  397.5 7.5 %collective-permute-start = (f32[512,128]{0,1:T(8,128)}, f32[512,128]{0,1:T(8,128)}, u32[]{:S(2)}, u32[]{:S(2)}) collective-permute-start(f32[512,128]{0,1:T(8,128)} %get-tuple-element.479), channel_id=1, source_target_pairs={{1,0},{2,1},{3,2},{4,3},{5,4},{6,5},{7,6},{9,8},{10,9},{11,10},{12... | collective-permute-start | bytes 786440 | tf_op jit(solution)/shard_map/while/body/eval_jaxpr/ppermute | solution.py:21
  403.7 3.6 collective-permute-start.1
  407.3 4.2 copy-start.1
  408.5 4.2 copy-start
  415.7 2.5 copy-start.2
  420.6 1.0 copy-start.3
  422.3 3.3 collective-permute-start
  424.3 3.6 collective-permute-start.1
Sparse Core Ops, SparseCore 0:
  11.9 165.5 all-gather.1
where the time goes:
time: 439 us; the launch traced here: 437 us
  waiting for transfers between devices  204 us (46%)
  starting transfers between devices  144 us (33%)
  local copies, waits for them, and re-layouts  33.4 us (8%)
  matrix products  22.5 us (5%)
  other arithmetic  19.3 us (4%)
  between operations  13.4 us (3%)
    all_gather x1, waiting for transfers between devices, rows_first(): filled, at, outs = (lax.all_gather(both, axis, axis=0, tiled=True), 0, [])  166 us
    ppermute x20, starting transfers between devices, shifted(): return lax.ppermute(value, axis, pairs)  144 us
    ppermute x20, waiting for transfers between devices, shifted(): return lax.ppermute(value, axis, pairs)  37.9 us
    dynamic_update_slice x10, other arithmetic, advance(): lax.dynamic_update_slice(matrix, jnp.where(landing, arrived, current), (h...  17.1 us
    dot_general x4, matrix products, reflect(): jnp.dot(basis_cols, coeffs, precision=highest, preferred_element_type=jnp...  9.19 us
  transfers between devices with their start and end apart: 21, of which 11 were waited for; matrix products, arithmetic and copies ran while one was open for 5% of the time, Pallas kernels for 0%

commit v1 on v0

v1 whole, which is shorter than its diff:
```python
import jax
import jax.numpy as jnp
from jax import lax
from jax.experimental import pallas as pl
from jax.experimental.pallas import tpu as pltpu
from jax.sharding import PartitionSpec as P

MESH = pl.DeviceIdType.MESH
F32, BF16 = jnp.float32, jnp.bfloat16
NZ, NX, NH = 8, 4, 2
B, HALF, N = 512, 256, 256
BAND = 640
LC = 128
STRIPES = B // LC
NN = (((1,), (0,)), ((), ()))
NT = (((1,), (1,)), ((), ()))
TN = (((0,), (0,)), ((), ()))


def split(v):
    hi = v.astype(BF16)
    return hi, (v - hi.astype(F32)).astype(BF16)


def dot3(a, b, dims=NN):
    def one(u, v):
        return lax.dot_general(u, v, dims, preferred_element_type=F32)

    return one(a[0], b[0]) + one(a[0], b[1]) + one(a[1], b[0])


def put(ref, at, v):
    hi, lo = split(v)
    ref[(0, *at)] = hi
    ref[(1, *at)] = lo


def get(ref, rows, cols):
    return ref[0, rows, cols], ref[1, rows, cols]


ALL, T0, T1 = slice(0, 512), slice(0, 256), slice(256, 512)


def times_lower(a, m, off=0):
    lo, hi = slice(off, off + 256), slice(off + 256, off + 512)
    left = dot3(get(a, slice(None), ALL), get(m, ALL, lo))
    right = dot3(get(a, slice(None), T1), get(m, T1, hi))
    return left, right


def times_upper(a, m):
    left = dot3(get(a, slice(None), T0), get(m, T0, T0))
    right = dot3(get(a, slice(None), ALL), get(m, ALL, T1))
    return left, right


def lower_lower(out, a, m, off=0):
    lo, hi = slice(off, off + 256), slice(off + 256, off + 512)
    put(out, (T0, T0), dot3(get(a, T0, T0), get(m, T0, lo)))
    put(out, (T1, T0), dot3(get(a, T1, ALL), get(m, ALL, lo)))
    put(out, (T1, T1), dot3(get(a, T1, T1), get(m, T1, hi)))


def kernel(
    vec, rft, fat, out,
    vt_buf, ft_buf, x_buf, xp_buf, d_buf, do_buf, ret_buf, ro_buf,
    xs, vs1, vs2, fs1, fs2, h1, h2, g, m, at, ds, ws, zs1, zs2,
    c1, c2, e, xt,
    lsem, p_s, p_r, vz_s, vz_r, vx_s, vx_r, fx_s, fx_r, fz_s, fz_r,
    xc_s, xc_r, d_s, d_r, ret_s, ret_r,
):
    c = lax.axis_index("cols")
    r = lax.axis_index("rows")
    z, x, h = c // (NX * NH), (c // NH) % NX, c % NH
    q = z // 2
    last = lax.axis_size("rows") - 1

    def at_c(zz, xx, hh):
        return (zz * NX + xx) * NH + hh

    zp, zm = at_c((z + 1) % NZ, x, h), at_c((z + NZ - 1) % NZ, x, h)
    xp, xm = at_c(z, (x + 1) % NX, h), at_c(z, (x + NX - 1) % NX, h)
    twin = at_c(z, x, 1 - h)
    b_first, b_own = jnp.maximum(2 * r - 1, 0), 2 * r
    zdir, xdir = (zp, zm), (xp, xm)

    own8 = pl.ds(pl.multiple_of(16 * x + 8 * h, 8), 8)
    lanes = pl.ds(pl.multiple_of(128 * q, 128), BAND)
    local = []
    for i, b in enumerate((b_first, b_own)):
        local.append(pltpu.make_async_copy(rft.at[b, :, lanes], vt_buf.at[i, z, own8, :], lsem.at[2 * i]))
        local.append(pltpu.make_async_copy(fat.at[b], ft_buf.at[i, z, own8, :], lsem.at[2 * i + 1]))
    xload = pltpu.make_async_copy(vec, x_buf, lsem.at[4])
    for cp in local:
        cp.start()
    xload.start()

    barrier = pltpu.get_barrier_semaphore()
    for cc in (zp, zm, xp, xm, twin):
        pl.semaphore_signal(barrier, inc=1, device_id=(cc, r), device_id_type=MESH)

    @pl.when(r > 0)
    def _():
        pl.semaphore_signal(barrier, inc=1, device_id=(c, r - 1), device_id_type=MESH)

    @pl.when(r < last)
    def _():
        pl.semaphore_signal(barrier, inc=1, device_id=(c, r + 1), device_id_type=MESH)

    pl.semaphore_wait(barrier, 5 + jnp.minimum(r, 1) + jnp.minimum(last - r, 1))

    sent = []

    def send(src, ssem, rsem, cc, rr=None, dst=None):
        cp = pltpu.make_async_remote_copy(
            src_ref=src, dst_ref=src if dst is None else dst, send_sem=ssem, recv_sem=rsem,
            device_id=(cc, r if rr is None else rr), device_id_type=MESH,
        )
        cp.start()
        sent.append(cp)

    def arrived(ref, ssem, rsem, cc):
        pltpu.make_async_remote_copy(
            src_ref=ref, dst_ref=ref, send_sem=ssem, recv_sem=rsem,
            device_id=(cc, r), device_id_type=MESH,
        ).wait_recv()

    for cp in local:
        cp.wait()
    send(vt_buf.at[:, z, own8, :], p_s.at[0], p_r.at[0], twin)
    send(ft_buf.at[:, z, own8, :], p_s.at[1], p_r.at[1], twin)
    xload.wait()

    @pl.when(r < last)
    def _():
        pltpu.make_async_remote_copy(
            src_ref=x_buf.at[pl.ds(B, B), :], dst_ref=xp_buf, send_sem=xc_s.at[0], recv_sem=xc_r.at[0],
            device_id=(c, r + 1), device_id_type=MESH,
        ).start()

    @pl.when(r == 0)
    def _():
        xp_buf[...] = jnp.zeros_like(xp_buf)
        d_buf[...] = jnp.zeros_like(d_buf)

    @pl.when(r == last)
    def _():
        ret_buf[...] = jnp.zeros_like(ret_buf)

    def rows16(xx):
        return pl.ds(pl.multiple_of(16 * xx, 16), 16)

    def vpiece(dz, xx, blk=slice(None)):
        return vt_buf.at[blk, (z + dz + NZ) % NZ, rows16(xx), :]

    def fslab(dz, blk):
        return ft_buf.at[blk, (z + dz + NZ) % NZ]

    def part(d):
        return pl.ds(d, 1)

    xnear = ((x + NX - 1) % NX, (x + 1) % NX)
    xfar = (x + 2) % NX
    other8 = pl.ds(pl.multiple_of(16 * x + 8 * (1 - h), 8), 8)

    def vz_send(s):
        for d in range(2):
            dz = -(s - 1) if d == 0 else s - 1
            ref = vpiece(dz, x) if s < 4 else vpiece(dz, x, part(d))
            send(ref, vz_s.at[d, s - 1], vz_r.at[d, s - 1], zdir[d])

    def vz_wait(s):
        for d in range(2):
            dz = -s if d == 0 else s
            ref = vpiece(dz, x) if s < 4 else vpiece(dz, x, part(d))
            arrived(ref, vz_s.at[d, s - 1], vz_r.at[d, s - 1], zdir[d])

    def vx_send1(dz):
        k = dz % NZ
        for d in range(2):
            send(vpiece(dz, x), vx_s.at[d, 0, k], vx_r.at[d, 0, k], xdir[d])

    def vx_send2(dz):
        k = dz % NZ
        for d in range(2):
            arrived(vpiece(dz, xnear[d]), vx_s.at[d, 0, k], vx_r.at[d, 0, k], xdir[d])
            send(vpiece(dz, xnear[d], part(d)), vx_s.at[d, 1, k], vx_r.at[d, 1, k], xdir[d])

    def vx_last(dz):
        k = dz % NZ
        for d in range(2):
            arrived(vpiece(dz, xfar, part(d)), vx_s.at[d, 1, k], vx_r.at[d, 1, k], xdir[d])

    def fz_send(s):
        for d in range(2):
            dz = -(s - 1) if d == 0 else s - 1
            for b in range(2) if s < 4 else (d,):
                send(fslab(dz, b), fz_s.at[d, b, s - 1], fz_r.at[d, b, s - 1], zdir[d])

    def fz_step(s):
        for b in range(2):
            for d in range(2):
                if s == 4 and b != d:
                    continue
                arrived(
                    fslab(-s if d == 0 else s, b), fz_s.at[d, b, s - 1], fz_r.at[d, b, s - 1], zdir[d]
                )
                if s < 3 or (s == 3 and b == d):
                    send(
                        fslab(-s if d == 0 else s, b), fz_s.at[d, b, s], fz_r.at[d, b, s], zdir[d]
                    )

    def fpiece(xx, blk=slice(None)):
        return ft_buf.at[blk, z, rows16(xx), :]

    arrived(vt_buf.at[:, z, other8, :], p_s.at[0], p_r.at[0], twin)
    vz_send(1)
    arrived(ft_buf.at[:, z, other8, :], p_s.at[1], p_r.at[1], twin)
    for d in range(2):
        send(fpiece(x), fx_s.at[d, 0], fx_r.at[d, 0], xdir[d])
    vx_send1(0)
    for d in range(2):
        arrived(fpiece(xnear[d]), fx_s.at[d, 0], fx_r.at[d, 0], xdir[d])
        send(fpiece(xnear[d], part(d)), fx_s.at[d, 1], fx_r.at[d, 1], xdir[d])
    vz_wait(1)
    vz_send(2)
    vx_send1(-1)
    vx_send1(1)
    for d in range(2):
        arrived(fpiece(xfar, part(d)), fx_s.at[d, 1], fx_r.at[d, 1], xdir[d])
    fz_send(1)
    vz_wait(2)
    vz_send(3)
    vx_send1(-2)
    vx_send1(2)
    vx_send2(0)
    vz_wait(3)
    vz_send(4)
    vx_send1(-3)
    vx_send1(3)
    fz_step(1)
    vx_send2(-1)
    vx_send2(1)
    vz_wait(4)
    vx_send1(4)
    fz_step(2)
    vx_send2(-2)
    vx_send2(2)

    @pl.when(r > 0)
    def _():
        pltpu.make_async_remote_copy(
            src_ref=x_buf.at[pl.ds(B, B), :], dst_ref=xp_buf, send_sem=xc_s.at[0], recv_sem=xc_r.at[0],
            device_id=(c, r), device_id_type=MESH,
        ).wait_recv()

    for i in range(4):
        rows = pl.ds(256 * i, 256)
        v = x_buf[rows, :].T
        xt[:, rows] = v
        put(xs, (slice(None), pl.ds(B + 256 * i, 256)), v)
    for i in range(2):
        put(xs, (slice(None), pl.ds(256 * i, 256)), xp_buf[pl.ds(256 * i, 256), :].T)

    fz_step(3)
    for dz in (-3, 3, 4):
        vx_send2(dz)
    for dz in (0, -1, 1, -2, 2, -3, 3, 4):
        vx_last(dz)

    has_upper = r > 0
    for vs, i in ((vs1, 0), (vs2, 1)):
        for qq in range(4):
            v = vt_buf[i, pl.ds(2 * qq, 2)].reshape(128, BAND)
            if i == 0:
                v = jnp.where(has_upper, v, jnp.zeros_like(v))
            rows = pl.ds(128 * qq, 128)
            put(vs, (rows, pl.ds(128 * qq, BAND)), v)
            gap = (640, 0, 896, 256)[qq]
            for k in range(2):
                vs[k, rows, pl.ds(gap, 128)] = jnp.zeros((128, 128), BF16)

    for cref, vs, off in ((c1, vs1, 0), (c2, vs2, B)):
        for a in range(2):
            w = pl.ds(256 * a, 768)
            cref[:, pl.ds(256 * a, 256)] = dot3(
                get(xs, slice(None), pl.ds(off + 256 * a, 768)), get(vs, pl.ds(256 * a, 256), w), NT
            )
    put(ws, (slice(None), slice(None)), c1[...])

    fz_step(4)
    for fs, i in ((fs1, 0), (fs2, 1)):
        for a in range(2):
            put(fs, (pl.ds(256 * a, 256), slice(None)), ft_buf[i, pl.ds(4 * a, 4)].reshape(256, B))

    lower_lower(h1, fs1, vs1, B)
    lower_lower(h2, fs2, vs2, B)
    put(g, (T0, T0), dot3(get(h1, T0, T0), get(vs2, T0, T0), NT))
    put(g, (T1, T0), dot3(get(h1, T1, ALL), get(vs2, T0, ALL), NT))
    put(g, (T1, T1), dot3(get(h1, T1, T1), get(vs2, T1, T1), NT))
    lower_lower(m, g, h2)
    put(at, (T0, T0), dot3(get(vs1, T0, T0), get(m, T0, T0), TN))
    put(at, (T1, T0), dot3(get(vs1, ALL, T1), get(m, ALL, T0), TN))
    put(at, (T1, T1), dot3(get(vs1, T1, T1), get(m, T1, T1), TN))
    for k in range(2):
        at[k, T0, T1] = jnp.zeros((256, 256), BF16)
    left, right = times_lower(ws, g)
    put(ds, (slice(None), T0), c2[:, T0] - left)
    put(ds, (slice(None), T1), c2[:, T1] - right)
    left, right = times_lower(ds, h2)
    e[:, T0] = left
    e[:, T1] = right

    def d_copy(i, rr):
        return pltpu.make_async_remote_copy(
            src_ref=do_buf.at[i], dst_ref=d_buf.at[i], send_sem=d_s.at[i], recv_sem=d_r.at[i],
            device_id=(c, rr), device_id_type=MESH,
        )

    for i in reversed(range(STRIPES)):
        @pl.when(r > 0)
        def _(i=i):
            d_copy(i, r).wait_recv()

        stripe, rest = slice(LC * i, LC * (i + 1)), slice(LC * i, B)
        put(ds, (slice(None), stripe), d_buf[i])
        do_buf[i] = e[:, stripe] + dot3(get(ds, slice(None), rest), get(at, rest, stripe))

        @pl.when(r < last)
        def _(i=i):
            d_copy(i, r + 1).start()

    put(ws, (slice(None), T1), c1[:, T1] - dot3(get(ds, slice(None), T1), get(vs1, T1, T1), NT))
    put(ws, (slice(None), T0), c1[:, T0] - dot3(get(ds, slice(None), ALL), get(vs1, T0, ALL), NT))
    left, right = times_lower(ws, fs1)
    put(zs1, (slice(None), T0), left)
    put(zs1, (slice(None), T1), right)

    def ret_copy(i, rr):
        return pltpu.make_async_remote_copy(
            src_ref=ro_buf.at[i], dst_ref=ret_buf.at[i], send_sem=ret_s.at[i], recv_sem=ret_r.at[i],
            device_id=(c, rr), device_id_type=MESH,
        )

    left, right = times_upper(zs1, vs1)
    for i, v in enumerate((left, right)):
        ro_buf[i] = v

        @pl.when(r > 0)
        def _(i=i):
            ret_copy(i, r - 1).start()

    left, right = times_lower(ws, g)
    put(ds, (slice(None), T0), c2[:, T0] - left)
    put(ds, (slice(None), T1), c2[:, T1] - right)
    left, right = times_lower(ds, fs2)
    put(zs2, (slice(None), T0), left)
    put(zs2, (slice(None), T1), right)
    low = times_lower(zs1, vs1, B)
    upp = times_upper(zs2, vs2)
    for i in range(2):
        cols = slice(256 * i, 256 * (i + 1))
        out[pl.ds(256 * i, 256), :] = (xt[:, cols] - low[i] - upp[i]).T

    for i in range(2):
        @pl.when(r < last)
        def _(i=i):
            ret_copy(i, r).wait_recv()

        for j in range(256 // LC):
            k = i * (256 // LC) + j
            lanes_k = slice(B + LC * k, B + LC * (k + 1))
            v = xt[:, lanes_k] - do_buf[k] - ret_buf[i, :, slice(LC * j, LC * (j + 1))]
            out[pl.ds(B + LC * k, LC), :] = v.T

    for cp in sent:
        cp.wait_send()

    @pl.when(r < last)
    def _():
        pltpu.make_async_remote_copy(
            src_ref=x_buf.at[pl.ds(B, B), :], dst_ref=xp_buf, send_sem=xc_s.at[0], recv_sem=xc_r.at[0],
            device_id=(c, r + 1), device_id_type=MESH,
        ).wait_send()
        for i in range(STRIPES):
            d_copy(i, r + 1).wait_send()

    @pl.when(r > 0)
    def _():
        for i in range(2):
            ret_copy(i, r - 1).wait_send()


def body(vectors, reflectors, factors):
    vmem = pltpu.VMEM
    dma = pltpu.SemaphoreType.DMA
    pair = (2, N, B)
    square = (2, B, B)
    scratch = [
        vmem((2, NZ, 64, BAND), F32), vmem((2, NZ, 64, B), F32),
        vmem((2 * B, N), F32), vmem((B, N), F32),
        vmem((STRIPES, N, LC), F32), vmem((STRIPES, N, LC), F32),
        vmem((2, N, HALF), F32), vmem((2, N, HALF), F32),
        vmem((2, N, 3 * B), BF16),
        vmem((2, B, 2 * B), BF16), vmem((2, B, 2 * B), BF16),
        vmem(square, BF16), vmem(square, BF16),
        vmem(square, BF16), vmem(square, BF16), vmem(square, BF16), vmem(square, BF16), vmem(square, BF16),
        vmem(pair, BF16), vmem(pair, BF16), vmem(pair, BF16), vmem(pair, BF16),
        vmem((N, B), F32), vmem((N, B), F32), vmem((N, B), F32), vmem((N, 2 * B), F32),
        dma((5,)), dma((2,)), dma((2,)), dma((2, 4)), dma((2, 4)), dma((2, 2, NZ)), dma((2, 2, NZ)),
        dma((2, 2)), dma((2, 2)), dma((2, 2, 4)), dma((2, 2, 4)),
        dma((1,)), dma((1,)), dma((STRIPES,)), dma((STRIPES,)), dma((2,)), dma((2,)),
    ]
    return pl.pallas_call(
        kernel,
        out_shape=jax.ShapeDtypeStruct((2 * B, N), F32),
        in_specs=[pl.BlockSpec(memory_space=pl.ANY)] * 3,
        out_specs=pl.BlockSpec(memory_space=pltpu.VMEM),
        scratch_shapes=scratch,
        compiler_params=pltpu.CompilerParams(
            collective_id=0, has_side_effects=True, vmem_limit_bytes=56 << 20
        ),
    )(vectors, jnp.transpose(reflectors, (0, 2, 1)), jnp.transpose(factors, (0, 2, 1)))


def solution(mesh):
    placed = (P("rows", "cols"), P(None, None, "cols"), P(None, None, "cols"))
    return jax.shard_map(
        body, mesh=mesh, in_specs=placed, out_specs=P("rows", "cols"), check_vma=False
    )
```

time: 439 us -> 93.3 us (0.21)
  the two profiles are of different devices: /device:TPU:27 before, /device:TPU:49 now
where the time goes in v1:
time: 93.3 us; the launch traced here: 93.1 us
  Pallas kernels  90.8 us (97%)
  local copies, waits for them, and re-layouts  2.26 us (2%)
    pallas_call x1, Pallas kernels, body(): pl.pallas_call(kernel, out_shape=jax.ShapeDtypeStruct((2 * B, N), F32), i...  90.8 us
    unnamed x1, local copies, waits for them, and re-layouts  2.26 us

profile of v1, /device:TPU:49, one launch (start us, length us, event | category | flops | bytes accessed | tf_op | source)
XLA Modules:
  0.0 93.1 jit_solution(16073386226568537318)
XLA Ops:
  0.0 90.8 %shard_map.37 = f32[1024,256]{1,0:T(8,128)} custom-call(f32[1024,256]{1,0:T(8,128)} %vec.1, f32[15,8,1024]{2,1,0:T(8,128)} %bitcast.2, f32[15,8,512]{2,1,0:T(8,128)} %bitcast.3), custom_call_target="tpu_custom_call" | custom-call | tf_op jit(solution)/shard_map/pallas_call | solution.py:415
  90.9 2.3 %copy.5 = f32[1024,256]{1,0:T(8,128)} copy(f32[1024,256]{1,0:T(8,128)} %shard_map.37) | data formatting | bytes 2097152

commit v2 on v1

--- a/solution.py
+++ b/solution.py
@@ -67,7 +67,7 @@
     vt_buf, ft_buf, x_buf, xp_buf, d_buf, do_buf, ret_buf, ro_buf,
     xs, vs1, vs2, fs1, fs2, h1, h2, g, m, at, ds, ws, zs1, zs2,
     c1, c2, e, xt,
-    lsem, p_s, p_r, vz_s, vz_r, vx_s, vx_r, fx_s, fx_r, fz_s, fz_r,
+    lsem, p_s, p_r, vz_s, vz_r, vx_s, vx_r, wx_s, wx_r, wz_s, wz_r, fx_s, fx_r, fz_s, fz_r,
     xc_s, xc_r, d_s, d_r, ret_s, ret_r,
 ):
     c = lax.axis_index("cols")
@@ -85,12 +85,11 @@
     b_first, b_own = jnp.maximum(2 * r - 1, 0), 2 * r
     zdir, xdir = (zp, zm), (xp, xm)
 
-    own8 = pl.ds(pl.multiple_of(16 * x + 8 * h, 8), 8)
     lanes = pl.ds(pl.multiple_of(128 * q, 128), BAND)
     local = []
     for i, b in enumerate((b_first, b_own)):
-        local.append(pltpu.make_async_copy(rft.at[b, :, lanes], vt_buf.at[i, z, own8, :], lsem.at[2 * i]))
-        local.append(pltpu.make_async_copy(fat.at[b], ft_buf.at[i, z, own8, :], lsem.at[2 * i + 1]))
+        local.append(pltpu.make_async_copy(rft.at[b, :, lanes], vt_buf.at[i, z, x, h], lsem.at[2 * i]))
+        local.append(pltpu.make_async_copy(fat.at[b], ft_buf.at[i, z, x, h], lsem.at[2 * i + 1]))
     xload = pltpu.make_async_copy(vec, x_buf, lsem.at[4])
     for cp in local:
         cp.start()
@@ -108,166 +107,232 @@
     def _():
         pl.semaphore_signal(barrier, inc=1, device_id=(c, r + 1), device_id_type=MESH)
 
-    pl.semaphore_wait(barrier, 5 + jnp.minimum(r, 1) + jnp.minimum(last - r, 1))
-
-    sent = []
-
-    def send(src, ssem, rsem, cc, rr=None, dst=None):
-        cp = pltpu.make_async_remote_copy(
-            src_ref=src, dst_ref=src if dst is None else dst, send_sem=ssem, recv_sem=rsem,
-            device_id=(cc, r if rr is None else rr), device_id_type=MESH,
-        )
-        cp.start()
-        sent.append(cp)
-
-    def arrived(ref, ssem, rsem, cc):
-        pltpu.make_async_remote_copy(
-            src_ref=ref, dst_ref=ref, send_sem=ssem, recv_sem=rsem,
-            device_id=(cc, r), device_id_type=MESH,
-        ).wait_recv()
-
+    @pl.when(r == 0)
+    def _():
+        xp_buf[...] = jnp.zeros_like(xp_buf)
+        d_buf[...] = jnp.zeros_like(d_buf)
+
+    @pl.when(r == last)
+    def _():
+        ret_buf[...] = jnp.zeros_like(ret_buf)
+
+    for i in range(2):
+        vs = (vs1, vs2)[i]
+        for qq in range(4):
+            gap = (640, 0, 896, 256)[qq]
+            for k in range(2):
+                vs[k, pl.ds(128 * qq, 128), pl.ds(gap, 128)] = jnp.zeros((128, 128), BF16)
+    for ref in (fs1, fs2):
+        for k in range(2):
+            ref[k, pl.ds(0, 128), pl.ds(128, 128)] = jnp.zeros((128, 128), BF16)
+            ref[k, pl.ds(256, 128), pl.ds(384, 128)] = jnp.zeros((128, 128), BF16)
     for cp in local:
         cp.wait()
-    send(vt_buf.at[:, z, own8, :], p_s.at[0], p_r.at[0], twin)
-    send(ft_buf.at[:, z, own8, :], p_s.at[1], p_r.at[1], twin)
     xload.wait()
-
-    @pl.when(r < last)
-    def _():
-        pltpu.make_async_remote_copy(
-            src_ref=x_buf.at[pl.ds(B, B), :], dst_ref=xp_buf, send_sem=xc_s.at[0], recv_sem=xc_r.at[0],
-            device_id=(c, r + 1), device_id_type=MESH,
-        ).start()
-
-    @pl.when(r == 0)
-    def _():
-        xp_buf[...] = jnp.zeros_like(xp_buf)
-        d_buf[...] = jnp.zeros_like(d_buf)
-
-    @pl.when(r == last)
-    def _():
-        ret_buf[...] = jnp.zeros_like(ret_buf)
-
-    def rows16(xx):
-        return pl.ds(pl.multiple_of(16 * xx, 16), 16)
-
-    def vpiece(dz, xx, blk=slice(None)):
-        return vt_buf.at[blk, (z + dz + NZ) % NZ, rows16(xx), :]
-
-    def fslab(dz, blk):
-        return ft_buf.at[blk, (z + dz + NZ) % NZ]
-
-    def part(d):
-        return pl.ds(d, 1)
-
-    xnear = ((x + NX - 1) % NX, (x + 1) % NX)
-    xfar = (x + 2) % NX
-    other8 = pl.ds(pl.multiple_of(16 * x + 8 * (1 - h), 8), 8)
-
-    def vz_send(s):
-        for d in range(2):
-            dz = -(s - 1) if d == 0 else s - 1
-            ref = vpiece(dz, x) if s < 4 else vpiece(dz, x, part(d))
-            send(ref, vz_s.at[d, s - 1], vz_r.at[d, s - 1], zdir[d])
-
-    def vz_wait(s):
-        for d in range(2):
-            dz = -s if d == 0 else s
-            ref = vpiece(dz, x) if s < 4 else vpiece(dz, x, part(d))
-            arrived(ref, vz_s.at[d, s - 1], vz_r.at[d, s - 1], zdir[d])
-
-    def vx_send1(dz):
-        k = dz % NZ
-        for d in range(2):
-            send(vpiece(dz, x), vx_s.at[d, 0, k], vx_r.at[d, 0, k], xdir[d])
-
-    def vx_send2(dz):
-        k = dz % NZ
-        for d in range(2):
-            arrived(vpiece(dz, xnear[d]), vx_s.at[d, 0, k], vx_r.at[d, 0, k], xdir[d])
-            send(vpiece(dz, xnear[d], part(d)), vx_s.at[d, 1, k], vx_r.at[d, 1, k], xdir[d])
-
-    def vx_last(dz):
-        k = dz % NZ
-        for d in range(2):
-            arrived(vpiece(dz, xfar, part(d)), vx_s.at[d, 1, k], vx_r.at[d, 1, k], xdir[d])
-
-    def fz_send(s):
-        for d in range(2):
-            dz = -(s - 1) if d == 0 else s - 1
-            for b in range(2) if s < 4 else (d,):
-                send(fslab(dz, b), fz_s.at[d, b, s - 1], fz_r.at[d, b, s - 1], zdir[d])
-
-    def fz_step(s):
-        for b in range(2):
-            for d in range(2):
-                if s == 4 and b != d:
-                    continue
-                arrived(
-                    fslab(-s if d == 0 else s, b), fz_s.at[d, b, s - 1], fz_r.at[d, b, s - 1], zdir[d]
-                )
-                if s < 3 or (s == 3 and b == d):
-                    send(
-                        fslab(-s if d == 0 else s, b), fz_s.at[d, b, s], fz_r.at[d, b, s], zdir[d]
-                    )
-
-    def fpiece(xx, blk=slice(None)):
-        return ft_buf.at[blk, z, rows16(xx), :]
-
-    arrived(vt_buf.at[:, z, other8, :], p_s.at[0], p_r.at[0], twin)
-    vz_send(1)
-    arrived(ft_buf.at[:, z, other8, :], p_s.at[1], p_r.at[1], twin)
-    for d in range(2):
-        send(fpiece(x), fx_s.at[d, 0], fx_r.at[d, 0], xdir[d])
-    vx_send1(0)
-    for d in range(2):
-        arrived(fpiece(xnear[d]), fx_s.at[d, 0], fx_r.at[d, 0], xdir[d])
-        send(fpiece(xnear[d], part(d)), fx_s.at[d, 1], fx_r.at[d, 1], xdir[d])
-    vz_wait(1)
-    vz_send(2)
-    vx_send1(-1)
-    vx_send1(1)
-    for d in range(2):
-        arrived(fpiece(xfar, part(d)), fx_s.at[d, 1], fx_r.at[d, 1], xdir[d])
-    fz_send(1)
-    vz_wait(2)
-    vz_send(3)
-    vx_send1(-2)
-    vx_send1(2)
-    vx_send2(0)
-    vz_wait(3)
-    vz_send(4)
-    vx_send1(-3)
-    vx_send1(3)
-    fz_step(1)
-    vx_send2(-1)
-    vx_send2(1)
-    vz_wait(4)
-    vx_send1(4)
-    fz_step(2)
-    vx_send2(-2)
-    vx_send2(2)
-
-    @pl.when(r > 0)
-    def _():
-        pltpu.make_async_remote_copy(
-            src_ref=x_buf.at[pl.ds(B, B), :], dst_ref=xp_buf, send_sem=xc_s.at[0], recv_sem=xc_r.at[0],
-            device_id=(c, r), device_id_type=MESH,
-        ).wait_recv()
-
     for i in range(4):
         rows = pl.ds(256 * i, 256)
         v = x_buf[rows, :].T
         xt[:, rows] = v
         put(xs, (slice(None), pl.ds(B + 256 * i, 256)), v)
+
+    pl.semaphore_wait(barrier, 5 + jnp.minimum(r, 1) + jnp.minimum(last - r, 1))
+
+    sent = []
+
+    def remote(ref, ssem, rsem, cc):
+        return pltpu.make_async_remote_copy(
+            src_ref=ref, dst_ref=ref, send_sem=ssem, recv_sem=rsem,
+            device_id=(cc, r), device_id_type=MESH,
+        )
+
+    def send(ref, ssem, rsem, cc):
+        cp = remote(ref, ssem, rsem, cc)
+        cp.start()
+        sent.append(cp.wait_send)
+
+    def arrived(ref, ssem, rsem, cc):
+        remote(ref, ssem, rsem, cc).wait_recv()
+
+    def by_width(zz, do):
+        for w in range(4):
+            @pl.when(zz // 2 == w)
+            def _(w=w):
+                do(128 * (w + 1))
+
+    def slab(dz):
+        return (z + dz + NZ) % NZ
+
+    both = slice(None)
+    xnear = ((x + NX - 1) % NX, (x + 1) % NX)
+    xfar = (x + 2) % NX
+
+    def part(d):
+        return pl.ds(d, 1)
+
+    def vz_args(n, d, dz):
+        half = both if n < 4 else part(d)
+        return vt_buf.at[0, slab(dz), x, half], vz_s.at[d, n - 1], vz_r.at[d, n - 1], zdir[d]
+
+    def vz_send(n):
+        for d in range(2):
+            send(*vz_args(n, d, (1 - n) if d == 0 else (n - 1)))
+
+    def vz_step(n):
+        for d in range(2):
+            arrived(*vz_args(n, d, -n if d == 0 else n))
+            if n < 4:
+                send(*vz_args(n + 1, d, -n if d == 0 else n))
+
+    def vx_args(dz, n, d, xx):
+        half = both if n == 0 else part(d)
+        k = dz % NZ
+        return vt_buf.at[0, slab(dz), xx, half], vx_s.at[d, n, k], vx_r.at[d, n, k], xdir[d]
+
+    def wx_args(n, d, xx):
+        half = both if n == 0 else part(d)
+        return vt_buf.at[1, z, xx, half], wx_s.at[d, n], wx_r.at[d, n], xdir[d]
+
+    def wz_args(n, d, p, dz):
+        return vt_buf.at[1, slab(dz), pl.ds(2 * p, 2)], wz_s.at[d, p, n - 1], wz_r.at[d, p, n - 1], zdir[d]
+
+    def wz_step(n):
+        for p in range(2):
+            for d in range(2):
+                if n == 4 and p != d:
+                    continue
+                dz = -n if d == 0 else n
+                if n > 0:
+                    arrived(*wz_args(n, d, p, dz))
+                if n < 3 or (n == 3 and p == d):
+                    send(*wz_args(n + 1, d, p, dz))
+
+    def fz_args(n, d, dz):
+        blk = both if n < 4 else part(d)
+        return ft_buf.at[blk, slab(dz), x], fz_s.at[d, n - 1], fz_r.at[d, n - 1], zdir[d]
+
+    def fz_send(n):
+        for d in range(2):
+            send(*fz_args(n, d, (1 - n) if d == 0 else (n - 1)))
+
+    def fz_step(n):
+        for d in range(2):
+            arrived(*fz_args(n, d, -n if d == 0 else n))
+            if n < 4:
+                send(*fz_args(n + 1, d, -n if d == 0 else n))
+
+    def fx(dz, n, d, xx, do):
+        blk, k = both if n == 0 else part(d), dz % NZ
+
+        def at_width(width):
+            do(remote(
+                ft_buf.at[blk, slab(dz), xx, :, :, pl.ds(0, width)],
+                fx_s.at[d, n, k], fx_r.at[d, n, k], xdir[d],
+            ))
+
+        by_width(slab(dz), at_width)
+
+    def fx_go(dz, n, d, xx):
+        fx(dz, n, d, xx, lambda cp: cp.start())
+        sent.append(lambda: fx(dz, n, d, xx, lambda cp: cp.wait_send()))
+
+    def x_send1(*dzs):
+        for dz in dzs:
+            for d in range(2):
+                send(*vx_args(dz, 0, d, x))
+
+    def fx_send1(*dzs):
+        for dz in dzs:
+            for d in range(2):
+                fx_go(dz, 0, d, x)
+
+    def x_send2(*dzs):
+        for dz in dzs:
+            for d in range(2):
+                arrived(*vx_args(dz, 0, d, xnear[d]))
+                send(*vx_args(dz, 1, d, xnear[d]))
+
+    def fx_send2(*dzs):
+        for dz in dzs:
+            for d in range(2):
+                fx(dz, 0, d, xnear[d], lambda cp: cp.wait_recv())
+                fx_go(dz, 1, d, xnear[d])
+
+    def x_last(*dzs):
+        for dz in dzs:
+            for d in range(2):
+                arrived(*vx_args(dz, 1, d, xfar))
+
+    def fx_last(*dzs):
+        for dz in dzs:
+            for d in range(2):
+                fx(dz, 1, d, xfar, lambda cp: cp.wait_recv())
+
+    def twin_args(ref, k, hh):
+        return ref.at[both, z, x, hh], p_s.at[k], p_r.at[k], twin
+
+    send(*twin_args(vt_buf, 0, h))
+    send(*twin_args(ft_buf, 1, h))
+    arrived(*twin_args(vt_buf, 0, 1 - h))
+    for d in range(2):
+        send(*wx_args(0, d, x))
+    vz_send(1)
+    arrived(*twin_args(ft_buf, 1, 1 - h))
+    fz_send(1)
+    x_send1(0)
+    fx_send1(0)
+
+    @pl.when(r < last)
+    def _():
+        pltpu.make_async_remote_copy(
+            src_ref=x_buf.at[pl.ds(B, B), :], dst_ref=xp_buf, send_sem=xc_s.at[0], recv_sem=xc_r.at[0],
+            device_id=(c, r + 1), device_id_type=MESH,
+        ).start()
+
+    for d in range(2):
+        arrived(*wx_args(0, d, xnear[d]))
+        send(*wx_args(1, d, xnear[d]))
+    vz_step(1)
+    fz_step(1)
+    x_send1(-1, 1)
+    fx_send1(-1, 1)
+    for d in range(2):
+        arrived(*wx_args(1, d, xfar))
+    wz_step(0)
+    vz_step(2)
+    fz_step(2)
+    x_send1(-2, 2)
+    fx_send1(-2, 2)
+    x_send2(0)
+    fx_send2(0)
+    wz_step(1)
+    vz_step(3)
+    fz_step(3)
+    x_send1(-3, 3)
+    fx_send1(-3, 3)
+    x_send2(-1, 1)
+    fx_send2(-1, 1)
+    vz_step(4)
+    fz_step(4)
+    x_send1(4)
+    fx_send1(4)
+    wz_step(2)
+    x_send2(-2, 2)
+    fx_send2(-2, 2)
+    wz_step(3)
+    x_send2(-3, 3, 4)
+    fx_send2(-3, 3, 4)
+
+    @pl.when(r > 0)
+    def _():
+        pltpu.make_async_remote_copy(
+            src_ref=x_buf.at[pl.ds(B, B), :], dst_ref=xp_buf, send_sem=xc_s.at[0], recv_sem=xc_r.at[0],
+            device_id=(c, r), device_id_type=MESH,
+        ).wait_recv()
+
     for i in range(2):
         put(xs, (slice(None), pl.ds(256 * i, 256)), xp_buf[pl.ds(256 * i, 256), :].T)
-
-    fz_step(3)
-    for dz in (-3, 3, 4):
-        vx_send2(dz)
-    for dz in (0, -1, 1, -2, 2, -3, 3, 4):
-        vx_last(dz)
+    wz_step(4)
+    x_last(0, -1, 1, -2, 2, -3, 3, 4)
 
     has_upper = r > 0
     for vs, i in ((vs1, 0), (vs2, 1)):
@@ -277,9 +342,6 @@
                 v = jnp.where(has_upper, v, jnp.zeros_like(v))
             rows = pl.ds(128 * qq, 128)
             put(vs, (rows, pl.ds(128 * qq, BAND)), v)
-            gap = (640, 0, 896, 256)[qq]
-            for k in range(2):
-                vs[k, rows, pl.ds(gap, 128)] = jnp.zeros((128, 128), BF16)
 
     for cref, vs, off in ((c1, vs1, 0), (c2, vs2, B)):
         for a in range(2):
@@ -289,10 +351,12 @@
             )
     put(ws, (slice(None), slice(None)), c1[...])
 
-    fz_step(4)
+    fx_last(0, -1, 1, -2, 2, -3, 3, 4)
     for fs, i in ((fs1, 0), (fs2, 1)):
-        for a in range(2):
-            put(fs, (pl.ds(256 * a, 256), slice(None)), ft_buf[i, pl.ds(4 * a, 4)].reshape(256, B))
+        for qq in range(4):
+            w = pl.ds(0, 128 * (qq + 1))
+            v = ft_buf[i, pl.ds(2 * qq, 2), :, :, :, w].reshape(128, 128 * (qq + 1))
+            put(fs, (pl.ds(128 * qq, 128), w), v)
 
     lower_lower(h1, fs1, vs1, B)
     lower_lower(h2, fs2, vs2, B)
@@ -374,8 +438,8 @@
             v = xt[:, lanes_k] - do_buf[k] - ret_buf[i, :, slice(LC * j, LC * (j + 1))]
             out[pl.ds(B + LC * k, LC), :] = v.T
 
-    for cp in sent:
-        cp.wait_send()
+    for done in sent:
+        done()
 
     @pl.when(r < last)
     def _():
@@ -398,7 +462,7 @@
     pair = (2, N, B)
     square = (2, B, B)
     scratch = [
-        vmem((2, NZ, 64, BAND), F32), vmem((2, NZ, 64, B), F32),
+        vmem((2, NZ, NX, NH, 8, BAND), F32), vmem((2, NZ, NX, NH, 8, B), F32),
         vmem((2 * B, N), F32), vmem((B, N), F32),
         vmem((STRIPES, N, LC), F32), vmem((STRIPES, N, LC), F32),
         vmem((2, N, HALF), F32), vmem((2, N, HALF), F32),
@@ -410,6 +474,7 @@
         vmem((N, B), F32), vmem((N, B), F32), vmem((N, B), F32), vmem((N, 2 * B), F32),
         dma((5,)), dma((2,)), dma((2,)), dma((2, 4)), dma((2, 4)), dma((2, 2, NZ)), dma((2, 2, NZ)),
         dma((2, 2)), dma((2, 2)), dma((2, 2, 4)), dma((2, 2, 4)),
+        dma((2, 2, NZ)), dma((2, 2, NZ)), dma((2, 4)), dma((2, 4)),
         dma((1,)), dma((1,)), dma((STRIPES,)), dma((STRIPES,)), dma((2,)), dma((2,)),
     ]
     return pl.pallas_call(

time: 93.3 us -> 87.8 us (0.941)
  Pallas kernels: 90.8 us -> 85.4 us
    pallas_call x1, Pallas kernels: 90.8 us -> 85.4 us  [body(): pl.pallas_call(kernel, out_shape=jax.ShapeDtypeStruct((2 * B, N), F32), i...]
where the time goes in v2:
time: 87.8 us; the launch traced here: 87.7 us
  Pallas kernels  85.4 us (97%)
  local copies, waits for them, and re-layouts  2.26 us (3%)
    pallas_call x1, Pallas kernels, body(): pl.pallas_call(kernel, out_shape=jax.ShapeDtypeStruct((2 * B, N), F32), i...  85.4 us
    unnamed x1, local copies, waits for them, and re-layouts  2.26 us

profile of v2, /device:TPU:49, one launch (start us, length us, event | category | flops | bytes accessed | tf_op | source)
XLA Modules:
  0.0 87.7 jit_solution(15036860362114526074)
XLA Ops:
  0.0 85.4 %shard_map.37 = f32[1024,256]{1,0:T(8,128)} custom-call(f32[1024,256]{1,0:T(8,128)} %vec.1, f32[15,8,1024]{2,1,0:T(8,128)} %bitcast.2, f32[15,8,512]{2,1,0:T(8,128)} %bitcast.3), custom_call_target="tpu_custom_call" | custom-call | tf_op jit(solution)/shard_map/pallas_call | solution.py:480
  85.4 2.3 %copy.5 = f32[1024,256]{1,0:T(8,128)} copy(f32[1024,256]{1,0:T(8,128)} %shard_map.37) | data formatting | bytes 2097152

commit v3 on v2

--- a/solution.py
+++ b/solution.py
@@ -12,6 +12,8 @@
 BAND = 640
 LC = 128
 STRIPES = B // LC
+PARTS = 2
+NC = N // PARTS
 NN = (((1,), (0,)), ((), ()))
 NT = (((1,), (1,)), ((), ()))
 TN = (((0,), (0,)), ((), ()))
@@ -42,16 +44,16 @@
 ALL, T0, T1 = slice(0, 512), slice(0, 256), slice(256, 512)
 
 
-def times_lower(a, m, off=0):
+def times_lower(a, m, off=0, rows=slice(None)):
     lo, hi = slice(off, off + 256), slice(off + 256, off + 512)
-    left = dot3(get(a, slice(None), ALL), get(m, ALL, lo))
-    right = dot3(get(a, slice(None), T1), get(m, T1, hi))
+    left = dot3(get(a, rows, ALL), get(m, ALL, lo))
+    right = dot3(get(a, rows, T1), get(m, T1, hi))
     return left, right
 
 
-def times_upper(a, m):
-    left = dot3(get(a, slice(None), T0), get(m, T0, T0))
-    right = dot3(get(a, slice(None), ALL), get(m, ALL, T1))
+def times_upper(a, m, rows):
+    left = dot3(get(a, rows, T0), get(m, T0, T0))
+    right = dot3(get(a, rows, ALL), get(m, ALL, T1))
     return left, right
 
 
@@ -67,7 +69,7 @@
     vt_buf, ft_buf, x_buf, xp_buf, d_buf, do_buf, ret_buf, ro_buf,
     xs, vs1, vs2, fs1, fs2, h1, h2, g, m, at, ds, ws, zs1, zs2,
     c1, c2, e, xt,
-    lsem, p_s, p_r, vz_s, vz_r, vx_s, vx_r, wx_s, wx_r, wz_s, wz_r, fx_s, fx_r, fz_s, fz_r,
+    gv_buf, gf_buf, gsem, lsem, p_s, p_r, vz_s, vz_r, vx_s, vx_r, wx_s, wx_r, wz_s, wz_r, fx_s, fx_r, fz_s, fz_r,
     xc_s, xc_r, d_s, d_r, ret_s, ret_r,
 ):
     c = lax.axis_index("cols")
@@ -95,9 +97,42 @@
         cp.start()
     xload.start()
 
+    y, core = r // 2, r % 2
+    near = 2 * jnp.where(y < 2, 3, 0) + core
+    giver = (y == 0) | (y == 3)
+    takers = [2 * (jnp.where(y == 3, 0, 2) + t) + core for t in range(2)]
+
+    def gift(t, i):
+        b = 2 * takers[t] if i else jnp.maximum(2 * takers[t] - 1, 0)
+        return (
+            pltpu.make_async_copy(rft.at[b, :, lanes], gv_buf.at[t, i], gsem.at[t, i, 0]),
+            pltpu.make_async_copy(fat.at[b], gf_buf.at[t, i], gsem.at[t, i, 1]),
+        )
+
+    def given(t, k):
+        src, dst = (gv_buf, vt_buf) if k == 0 else (gf_buf, ft_buf)
+        return pltpu.make_async_remote_copy(
+            src_ref=src.at[t], dst_ref=dst.at[:, z, x, h], send_sem=p_s.at[t, k], recv_sem=p_r.at[k],
+            device_id=(twin, takers[t]), device_id_type=MESH,
+        )
+
+    @pl.when(giver)
+    def _():
+        for t in range(2):
+            for i in range(2):
+                for cp in gift(t, i):
+                    cp.start()
+
     barrier = pltpu.get_barrier_semaphore()
-    for cc in (zp, zm, xp, xm, twin):
+    for cc in (zp, zm, xp, xm):
         pl.semaphore_signal(barrier, inc=1, device_id=(cc, r), device_id_type=MESH)
+
+    pl.semaphore_signal(barrier, inc=1, device_id=(twin, near), device_id_type=MESH)
+
+    @pl.when(giver)
+    def _():
+        for t in range(2):
+            pl.semaphore_signal(barrier, inc=1, device_id=(twin, takers[t]), device_id_type=MESH)
 
     @pl.when(r > 0)
     def _():
@@ -135,7 +170,21 @@
         xt[:, rows] = v
         put(xs, (slice(None), pl.ds(B + 256 * i, 256)), v)
 
-    pl.semaphore_wait(barrier, 5 + jnp.minimum(r, 1) + jnp.minimum(last - r, 1))
+    @pl.when(giver)
+    def _():
+        for t in range(2):
+            for i in range(2):
+                for cp in gift(t, i):
+                    cp.wait()
+
+    peers = 5 + jnp.minimum(r, 1) + jnp.minimum(last - r, 1) + jnp.where(giver, 2, 0)
+    pl.semaphore_wait(barrier, peers)
+
+    @pl.when(giver)
+    def _():
+        for k in range(2):
+            for t in range(2):
+                given(t, k).start()
 
     sent = []
 
@@ -267,16 +316,11 @@
             for d in range(2):
                 fx(dz, 1, d, xfar, lambda cp: cp.wait_recv())
 
-    def twin_args(ref, k, hh):
-        return ref.at[both, z, x, hh], p_s.at[k], p_r.at[k], twin
-
-    send(*twin_args(vt_buf, 0, h))
-    send(*twin_args(ft_buf, 1, h))
-    arrived(*twin_args(vt_buf, 0, 1 - h))
+    arrived(vt_buf.at[:, z, x, 1 - h], p_s.at[0, 0], p_r.at[0], twin)
     for d in range(2):
         send(*wx_args(0, d, x))
     vz_send(1)
-    arrived(*twin_args(ft_buf, 1, 1 - h))
+    arrived(ft_buf.at[:, z, x, 1 - h], p_s.at[0, 1], p_r.at[1], twin)
     fz_send(1)
     x_send1(0)
     fx_send1(0)
@@ -376,70 +420,78 @@
     e[:, T0] = left
     e[:, T1] = right
 
-    def d_copy(i, rr):
+    def d_copy(j, i, rr):
         return pltpu.make_async_remote_copy(
-            src_ref=do_buf.at[i], dst_ref=d_buf.at[i], send_sem=d_s.at[i], recv_sem=d_r.at[i],
+            src_ref=do_buf.at[j, i], dst_ref=d_buf.at[j, i], send_sem=d_s.at[j, i], recv_sem=d_r.at[j, i],
             device_id=(c, rr), device_id_type=MESH,
         )
 
-    for i in reversed(range(STRIPES)):
-        @pl.when(r > 0)
-        def _(i=i):
-            d_copy(i, r).wait_recv()
-
-        stripe, rest = slice(LC * i, LC * (i + 1)), slice(LC * i, B)
-        put(ds, (slice(None), stripe), d_buf[i])
-        do_buf[i] = e[:, stripe] + dot3(get(ds, slice(None), rest), get(at, rest, stripe))
-
-        @pl.when(r < last)
-        def _(i=i):
-            d_copy(i, r + 1).start()
-
-    put(ws, (slice(None), T1), c1[:, T1] - dot3(get(ds, slice(None), T1), get(vs1, T1, T1), NT))
-    put(ws, (slice(None), T0), c1[:, T0] - dot3(get(ds, slice(None), ALL), get(vs1, T0, ALL), NT))
-    left, right = times_lower(ws, fs1)
-    put(zs1, (slice(None), T0), left)
-    put(zs1, (slice(None), T1), right)
-
-    def ret_copy(i, rr):
+    def ret_copy(j, rr):
         return pltpu.make_async_remote_copy(
-            src_ref=ro_buf.at[i], dst_ref=ret_buf.at[i], send_sem=ret_s.at[i], recv_sem=ret_r.at[i],
+            src_ref=ro_buf.at[j], dst_ref=ret_buf.at[j], send_sem=ret_s.at[j], recv_sem=ret_r.at[j],
             device_id=(c, rr), device_id_type=MESH,
         )
 
-    left, right = times_upper(zs1, vs1)
-    for i, v in enumerate((left, right)):
-        ro_buf[i] = v
+    for j in range(PARTS):
+        rows = slice(NC * j, NC * (j + 1))
+        for i in reversed(range(STRIPES)):
+            @pl.when(r > 0)
+            def _(i=i):
+                d_copy(j, i, r).wait_recv()
+
+            stripe, rest = slice(LC * i, LC * (i + 1)), slice(LC * i, B)
+            put(ds, (rows, stripe), d_buf[j, i])
+            do_buf[j, i] = e[rows, stripe] + dot3(get(ds, rows, rest), get(at, rest, stripe))
+
+            @pl.when(r < last)
+            def _(i=i):
+                d_copy(j, i, r + 1).start()
+
+        put(ws, (rows, T1), c1[rows, T1] - dot3(get(ds, rows, T1), get(vs1, T1, T1), NT))
+        put(ws, (rows, T0), c1[rows, T0] - dot3(get(ds, rows, ALL), get(vs1, T0, ALL), NT))
+        left, right = times_lower(ws, fs1, 0, rows)
+        put(zs1, (rows, T0), left)
+        put(zs1, (rows, T1), right)
+        left, right = times_upper(zs1, vs1, rows)
+        ro_buf[j, :, T0] = left
+        ro_buf[j, :, T1] = right
 
         @pl.when(r > 0)
-        def _(i=i):
-            ret_copy(i, r - 1).start()
-
-    left, right = times_lower(ws, g)
-    put(ds, (slice(None), T0), c2[:, T0] - left)
-    put(ds, (slice(None), T1), c2[:, T1] - right)
-    left, right = times_lower(ds, fs2)
-    put(zs2, (slice(None), T0), left)
-    put(zs2, (slice(None), T1), right)
-    low = times_lower(zs1, vs1, B)
-    upp = times_upper(zs2, vs2)
-    for i in range(2):
-        cols = slice(256 * i, 256 * (i + 1))
-        out[pl.ds(256 * i, 256), :] = (xt[:, cols] - low[i] - upp[i]).T
-
-    for i in range(2):
+        def _():
+            ret_copy(j, r - 1).start()
+
+        left, right = times_lower(ws, g, 0, rows)
+        put(ds, (rows, T0), c2[rows, T0] - left)
+        put(ds, (rows, T1), c2[rows, T1] - right)
+        left, right = times_lower(ds, fs2, 0, rows)
+        put(zs2, (rows, T0), left)
+        put(zs2, (rows, T1), right)
+        low = times_lower(zs1, vs1, B, rows)
+        upp = times_upper(zs2, vs2, rows)
+        for i in range(2):
+            cols = slice(256 * i, 256 * (i + 1))
+            out[pl.ds(256 * i, 256), pl.ds(NC * j, NC)] = (xt[rows, cols] - low[i] - upp[i]).T
+
+    for j in range(PARTS):
+        rows = slice(NC * j, NC * (j + 1))
+
         @pl.when(r < last)
-        def _(i=i):
-            ret_copy(i, r).wait_recv()
-
-        for j in range(256 // LC):
-            k = i * (256 // LC) + j
-            lanes_k = slice(B + LC * k, B + LC * (k + 1))
-            v = xt[:, lanes_k] - do_buf[k] - ret_buf[i, :, slice(LC * j, LC * (j + 1))]
-            out[pl.ds(B + LC * k, LC), :] = v.T
+        def _():
+            ret_copy(j, r).wait_recv()
+
+        for k in range(STRIPES):
+            stripe = slice(LC * k, LC * (k + 1))
+            v = xt[rows, slice(B + LC * k, B + LC * (k + 1))] - do_buf[j, k] - ret_buf[j, :, stripe]
+            out[pl.ds(B + LC * k, LC), pl.ds(NC * j, NC)] = v.T
 
     for done in sent:
         done()
+
+    @pl.when(giver)
+    def _():
+        for k in range(2):
+            for t in range(2):
+                given(t, k).wait_send()
 
     @pl.when(r < last)
     def _():
@@ -447,13 +499,14 @@
             src_ref=x_buf.at[pl.ds(B, B), :], dst_ref=xp_buf, send_sem=xc_s.at[0], recv_sem=xc_r.at[0],
             device_id=(c, r + 1), device_id_type=MESH,
         ).wait_send()
-        for i in range(STRIPES):
-            d_copy(i, r + 1).wait_send()
+        for j in range(PARTS):
+            for i in range(STRIPES):
+                d_copy(j, i, r + 1).wait_send()
 
     @pl.when(r > 0)
     def _():
-        for i in range(2):
-            ret_copy(i, r - 1).wait_send()
+        for j in range(PARTS):
+            ret_copy(j, r - 1).wait_send()
 
 
 def body(vectors, reflectors, factors):
@@ -464,18 +517,19 @@
     scratch = [
         vmem((2, NZ, NX, NH, 8, BAND), F32), vmem((2, NZ, NX, NH, 8, B), F32),
         vmem((2 * B, N), F32), vmem((B, N), F32),
-        vmem((STRIPES, N, LC), F32), vmem((STRIPES, N, LC), F32),
-        vmem((2, N, HALF), F32), vmem((2, N, HALF), F32),
+        vmem((PARTS, STRIPES, NC, LC), F32), vmem((PARTS, STRIPES, NC, LC), F32),
+        vmem((PARTS, NC, B), F32), vmem((PARTS, NC, B), F32),
         vmem((2, N, 3 * B), BF16),
         vmem((2, B, 2 * B), BF16), vmem((2, B, 2 * B), BF16),
         vmem(square, BF16), vmem(square, BF16),
         vmem(square, BF16), vmem(square, BF16), vmem(square, BF16), vmem(square, BF16), vmem(square, BF16),
         vmem(pair, BF16), vmem(pair, BF16), vmem(pair, BF16), vmem(pair, BF16),
         vmem((N, B), F32), vmem((N, B), F32), vmem((N, B), F32), vmem((N, 2 * B), F32),
-        dma((5,)), dma((2,)), dma((2,)), dma((2, 4)), dma((2, 4)), dma((2, 2, NZ)), dma((2, 2, NZ)),
+        vmem((2, 2, 8, BAND), F32), vmem((2, 2, 8, B), F32), dma((2, 2, 2)),
+        dma((5,)), dma((2, 2)), dma((2,)), dma((2, 4)), dma((2, 4)), dma((2, 2, NZ)), dma((2, 2, NZ)),
         dma((2, 2)), dma((2, 2)), dma((2, 2, 4)), dma((2, 2, 4)),
         dma((2, 2, NZ)), dma((2, 2, NZ)), dma((2, 4)), dma((2, 4)),
-        dma((1,)), dma((1,)), dma((STRIPES,)), dma((STRIPES,)), dma((2,)), dma((2,)),
+        dma((1,)), dma((1,)), dma((PARTS, STRIPES)), dma((PARTS, STRIPES)), dma((PARTS,)), dma((PARTS,)),
     ]
     return pl.pallas_call(
         kernel,

time: 87.8 us -> 81.4 us (0.927)
  the two profiles are of different devices: /device:TPU:49 before, /device:TPU:17 now
where the time goes in v3:
time: 81.4 us; the launch traced here: 81.2 us
  Pallas kernels  79 us (97%)
  local copies, waits for them, and re-layouts  2.26 us (3%)
    pallas_call x1, Pallas kernels, body(): pl.pallas_call(kernel, out_shape=jax.ShapeDtypeStruct((2 * B, N), F32), i...  79 us
    unnamed x1, local copies, waits for them, and re-layouts  2.26 us

profile of v3, /device:TPU:17, one launch (start us, length us, event | category | flops | bytes accessed | tf_op | source)
XLA Modules:
  0.0 81.2 jit_solution(4148324014207455182)
XLA Ops:
  0.0 79.0 %shard_map.37 = f32[1024,256]{1,0:T(8,128)} custom-call(f32[1024,256]{1,0:T(8,128)} %vec.1, f32[15,8,1024]{2,1,0:T(8,128)} %bitcast.2, f32[15,8,512]{2,1,0:T(8,128)} %bitcast.3), custom_call_target="tpu_custom_call" | custom-call | tf_op jit(solution)/shard_map/pallas_call | solution.py:534
  79.0 2.3 %copy.5 = f32[1024,256]{1,0:T(8,128)} copy(f32[1024,256]{1,0:T(8,128)} %shard_map.37) | data formatting | bytes 2097152

commit v4 on v3

--- a/solution.py
+++ b/solution.py
@@ -375,24 +375,30 @@
 
     for i in range(2):
         put(xs, (slice(None), pl.ds(256 * i, 256)), xp_buf[pl.ds(256 * i, 256), :].T)
-    wz_step(4)
-    x_last(0, -1, 1, -2, 2, -3, 3, 4)
-
     has_upper = r > 0
-    for vs, i in ((vs1, 0), (vs2, 1)):
+
+    def unpack(i):
+        vs = (vs1, vs2)[i]
         for qq in range(4):
             v = vt_buf[i, pl.ds(2 * qq, 2)].reshape(128, BAND)
             if i == 0:
                 v = jnp.where(has_upper, v, jnp.zeros_like(v))
-            rows = pl.ds(128 * qq, 128)
-            put(vs, (rows, pl.ds(128 * qq, BAND)), v)
-
-    for cref, vs, off in ((c1, vs1, 0), (c2, vs2, B)):
+            put(vs, (pl.ds(128 * qq, 128), pl.ds(128 * qq, BAND)), v)
+
+    def own_weights(i):
+        cref, vs, off = ((c1, vs1, 0), (c2, vs2, B))[i]
         for a in range(2):
             w = pl.ds(256 * a, 768)
             cref[:, pl.ds(256 * a, 256)] = dot3(
                 get(xs, slice(None), pl.ds(off + 256 * a, 768)), get(vs, pl.ds(256 * a, 256), w), NT
             )
+
+    wz_step(4)
+    unpack(1)
+    own_weights(1)
+    x_last(0, -1, 1, -2, 2, -3, 3, 4)
+    unpack(0)
+    own_weights(0)
     put(ws, (slice(None), slice(None)), c1[...])
 
     fx_last(0, -1, 1, -2, 2, -3, 3, 4)
@@ -434,6 +440,7 @@
 
     for j in range(PARTS):
         rows = slice(NC * j, NC * (j + 1))
+        acc = e[rows, slice(B - LC, B)]
         for i in reversed(range(STRIPES)):
             @pl.when(r > 0)
             def _(i=i):
@@ -441,11 +448,15 @@
 
             stripe, rest = slice(LC * i, LC * (i + 1)), slice(LC * i, B)
             put(ds, (rows, stripe), d_buf[j, i])
-            do_buf[j, i] = e[rows, stripe] + dot3(get(ds, rows, rest), get(at, rest, stripe))
+            do_buf[j, i] = acc + dot3(get(ds, rows, stripe), get(at, stripe, stripe))
 
             @pl.when(r < last)
             def _(i=i):
                 d_copy(j, i, r + 1).start()
+
+            if i > 0:
+                after = slice(LC * (i - 1), LC * i)
+                acc = e[rows, after] + dot3(get(ds, rows, rest), get(at, rest, after))
 
         put(ws, (rows, T1), c1[rows, T1] - dot3(get(ds, rows, T1), get(vs1, T1, T1), NT))
         put(ws, (rows, T0), c1[rows, T0] - dot3(get(ds, rows, ALL), get(vs1, T0, ALL), NT))
@@ -460,6 +471,8 @@
         def _():
             ret_copy(j, r - 1).start()
 
+    for j in range(PARTS):
+        rows = slice(NC * j, NC * (j + 1))
         left, right = times_lower(ws, g, 0, rows)
         put(ds, (rows, T0), c2[rows, T0] - left)
         put(ds, (rows, T1), c2[rows, T1] - right)

time: 81.4 us -> 79.3 us (0.974)
  Pallas kernels: 79 us -> 76.9 us
    pallas_call x1, Pallas kernels: 79 us -> 76.9 us  [body(): pl.pallas_call(kernel, out_shape=jax.ShapeDtypeStruct((2 * B, N), F32), i...]
where the time goes in v4:
time: 79.3 us; the launch traced here: 79.1 us
  Pallas kernels  76.9 us (97%)
  local copies, waits for them, and re-layouts  2.26 us (3%)
    pallas_call x1, Pallas kernels, body(): pl.pallas_call(kernel, out_shape=jax.ShapeDtypeStruct((2 * B, N), F32), i...  76.9 us
    unnamed x1, local copies, waits for them, and re-layouts  2.26 us

profile of v4, /device:TPU:17, one launch (start us, length us, event | category | flops | bytes accessed | tf_op | source)
XLA Modules:
  0.0 79.1 jit_solution(11457997414770096671)
XLA Ops:
  0.0 76.9 %shard_map.37 = f32[1024,256]{1,0:T(8,128)} custom-call(f32[1024,256]{1,0:T(8,128)} %vec.1, f32[15,8,1024]{2,1,0:T(8,128)} %bitcast.2, f32[15,8,512]{2,1,0:T(8,128)} %bitcast.3), custom_call_target="tpu_custom_call" | custom-call | tf_op jit(solution)/shard_map/pallas_call | solution.py:547
  76.9 2.3 %copy.5 = f32[1024,256]{1,0:T(8,128)} copy(f32[1024,256]{1,0:T(8,128)} %shard_map.37) | data formatting | bytes 2097152

commit v5 on v4

--- a/solution.py
+++ b/solution.py
@@ -413,30 +413,38 @@
     put(g, (T0, T0), dot3(get(h1, T0, T0), get(vs2, T0, T0), NT))
     put(g, (T1, T0), dot3(get(h1, T1, ALL), get(vs2, T0, ALL), NT))
     put(g, (T1, T1), dot3(get(h1, T1, T1), get(vs2, T1, T1), NT))
+    left, right = times_lower(ws, g)
+    put(ds, (slice(None), T0), c2[:, T0] - left)
+    put(ds, (slice(None), T1), c2[:, T1] - right)
+    left, right = times_lower(ds, h2)
+    e[:, T0] = left
+    e[:, T1] = right
+
+    def d_copy(j, i, rr):
+        return pltpu.make_async_remote_copy(
+            src_ref=do_buf.at[j, i], dst_ref=d_buf.at[j, i], send_sem=d_s.at[j, i], recv_sem=d_r.at[j, i],
+            device_id=(c, rr), device_id_type=MESH,
+        )
+
+    def ret_copy(j, rr):
+        return pltpu.make_async_remote_copy(
+            src_ref=ro_buf.at[j], dst_ref=ret_buf.at[j], send_sem=ret_s.at[j], recv_sem=ret_r.at[j],
+            device_id=(c, rr), device_id_type=MESH,
+        )
+
+    @pl.when(r == 0)
+    def _():
+        for j in range(PARTS):
+            for i in reversed(range(STRIPES)):
+                do_buf[j, i] = e[slice(NC * j, NC * (j + 1)), slice(LC * i, LC * (i + 1))]
+                d_copy(j, i, r + 1).start()
+
     lower_lower(m, g, h2)
     put(at, (T0, T0), dot3(get(vs1, T0, T0), get(m, T0, T0), TN))
     put(at, (T1, T0), dot3(get(vs1, ALL, T1), get(m, ALL, T0), TN))
     put(at, (T1, T1), dot3(get(vs1, T1, T1), get(m, T1, T1), TN))
     for k in range(2):
         at[k, T0, T1] = jnp.zeros((256, 256), BF16)
-    left, right = times_lower(ws, g)
-    put(ds, (slice(None), T0), c2[:, T0] - left)
-    put(ds, (slice(None), T1), c2[:, T1] - right)
-    left, right = times_lower(ds, h2)
-    e[:, T0] = left
-    e[:, T1] = right
-
-    def d_copy(j, i, rr):
-        return pltpu.make_async_remote_copy(
-            src_ref=do_buf.at[j, i], dst_ref=d_buf.at[j, i], send_sem=d_s.at[j, i], recv_sem=d_r.at[j, i],
-            device_id=(c, rr), device_id_type=MESH,
-        )
-
-    def ret_copy(j, rr):
-        return pltpu.make_async_remote_copy(
-            src_ref=ro_buf.at[j], dst_ref=ret_buf.at[j], send_sem=ret_s.at[j], recv_sem=ret_r.at[j],
-            device_id=(c, rr), device_id_type=MESH,
-        )
 
     for j in range(PARTS):
         rows = slice(NC * j, NC * (j + 1))
@@ -448,9 +456,13 @@
 
             stripe, rest = slice(LC * i, LC * (i + 1)), slice(LC * i, B)
             put(ds, (rows, stripe), d_buf[j, i])
-            do_buf[j, i] = acc + dot3(get(ds, rows, stripe), get(at, stripe, stripe))
-
-            @pl.when(r < last)
+            total = acc + dot3(get(ds, rows, stripe), get(at, stripe, stripe))
+
+            @pl.when(r > 0)
+            def _(i=i, total=total):
+                do_buf[j, i] = total
+
+            @pl.when((r > 0) & (r < last))
             def _(i=i):
                 d_copy(j, i, r + 1).start()
 

time: 79.3 us -> 78.9 us (level)
  no operation moved by 1% of the time
where the time goes in v5:
time: 78.9 us; the launch traced here: 78.8 us
  Pallas kernels  76.5 us (97%)
  local copies, waits for them, and re-layouts  2.26 us (3%)
    pallas_call x1, Pallas kernels, body(): pl.pallas_call(kernel, out_shape=jax.ShapeDtypeStruct((2 * B, N), F32), i...  76.5 us
    unnamed x1, local copies, waits for them, and re-layouts  2.26 us

profile of v5, /device:TPU:17, one launch (start us, length us, event | category | flops | bytes accessed | tf_op | source)
XLA Modules:
  0.0 78.8 jit_solution(8982002410115898343)
XLA Ops:
  0.0 76.5 %shard_map.37 = f32[1024,256]{1,0:T(8,128)} custom-call(f32[1024,256]{1,0:T(8,128)} %vec.1, f32[15,8,1024]{2,1,0:T(8,128)} %bitcast.2, f32[15,8,512]{2,1,0:T(8,128)} %bitcast.3), custom_call_target="tpu_custom_call" | custom-call | tf_op jit(solution)/shard_map/pallas_call | solution.py:559
  76.5 2.3 %copy.5 = f32[1024,256]{1,0:T(8,128)} copy(f32[1024,256]{1,0:T(8,128)} %shard_map.37) | data formatting | bytes 2097152
